TPU v7x, 32 devices: a whole 2x2x4 slice. The times are simulated.
32 devices in a mesh: seq: 4 (over z), tensor: 2 (over x), dp: 4 (over y, core).
Axes of the slice: x: 2, y: 2, z: 4, core: 2. Of those that a mesh axis runs over, the one named last changes fastest.
Arguments:
- tokens: bfloat16 [4, 1024, 3072], P('dp', 'seq'), may hold values from -6 to 6
- cotangent: bfloat16 [4, 1024, 3072], P('dp', 'seq'), may hold values from -6 to 6
- qkv_weight: bfloat16 [3072, 3, 768], P(('seq', 'dp'), None, 'tensor'), may hold values from -0.109375 to 0.109375
- out_weight: bfloat16 [3072, 768], P(('seq', 'dp'), 'tensor'), may hold values from -0.21875 to 0.21875
Outputs:
- qkv_grad: float32 [3072, 3, 768], P(('seq', 'dp'), None, 'tensor')
- out_grad: float32 [3072, 768], P(('seq', 'dp'), 'tensor')
- branch_grad: bfloat16 [4, 1024, 3072], P('dp', 'seq', 'tensor')
All inputs are finite; a program needn't handle non-finite values.
Results may differ from a plain program's by a relative error of at most 0.025.
Values may be sent and summed in bfloat16 or wider, within the bound.
A program may use at most 128 MiB of HBM per device.

v0:
```python
import jax
import jax.numpy as jnp
from jax import lax
from jax.sharding import PartitionSpec as P

HD = 128


epsilon = 1e-06


def normalize(values):
    average = jnp.mean(values, axis=-1, keepdims=True)
    centered = values - average
    inverse = lax.rsqrt(jnp.mean(centered * centered, axis=-1, keepdims=True) + epsilon)
    return (centered * inverse, inverse)


def normalize_back(gradient, normed, inverse):
    mean_grad = jnp.mean(gradient, axis=-1, keepdims=True)
    mean_both = jnp.mean(gradient * normed, axis=-1, keepdims=True)
    return (gradient - mean_grad - normed * mean_both) * inverse


def local(tokens, cotangent, qkv_weight, out_weight):
    row_count = tokens.shape[1]
    feature_count = tokens.shape[2]
    column_count = out_weight.shape[1]
    head_count = column_count // HD
    score_scale = HD ** (-0.5)
    own_rows = qkv_weight.shape[0]
    grad_rows = cotangent[0]
    normed, inverse = normalize(tokens[0].astype(jnp.float32))
    unit_low = normed.astype(jnp.bfloat16)
    flat_weight = qkv_weight.reshape(own_rows, 3 * column_count)
    piece_qkv = lax.all_gather(flat_weight, ("seq", "dp"), axis=0, tiled=True)
    piece_out = lax.all_gather(out_weight, ("seq", "dp"), axis=0, tiled=True)
    piece_rows = piece_qkv.shape[0]
    left_rows = unit_low
    right_rows = grad_rows
    projected = jnp.dot(left_rows, piece_qkv, preferred_element_type=jnp.float32)
    attended_grad = jnp.dot(right_rows, piece_out, preferred_element_type=jnp.float32)
    full_qkv = piece_qkv
    projected, attended_grad, full_qkv = (projected, attended_grad, full_qkv)
    query_unit, query_inv = normalize(
        projected[:, :column_count].reshape(row_count, head_count, HD)
    )
    key_unit, key_inv = normalize(
        projected[:, column_count : 2 * column_count].reshape(row_count, head_count, HD)
    )
    query_low = query_unit.astype(jnp.bfloat16)
    key_value = jnp.stack(
        [
            key_unit.astype(jnp.bfloat16).reshape(row_count, column_count),
            projected[:, 2 * column_count :].astype(jnp.bfloat16),
        ]
    )
    grad_low = attended_grad.astype(jnp.bfloat16).reshape(row_count, head_count, HD)

    def scores_of(key_rows):
        piece_rows = key_rows.shape[0]
        return (
            jnp.einsum(
                "qhd,khd->hqk",
                query_low,
                key_rows.reshape(piece_rows, head_count, HD),
                preferred_element_type=jnp.float32,
            )
            * score_scale
        )

    every_pair = lax.all_gather(key_value, "seq", axis=1, tiled=True)
    piece_rows = every_pair.shape[1]
    exponent = jnp.exp(scores_of(every_pair[0]))
    add_exp_total = jnp.sum(exponent, axis=-1)
    weighted = jnp.einsum(
        "hqk,khd->qhd",
        exponent.astype(jnp.bfloat16),
        every_pair[1].reshape(piece_rows, head_count, HD),
        preferred_element_type=jnp.float32,
    )
    exp_total, weighted = (add_exp_total, weighted)
    attended_low = (weighted / exp_total.T[:, :, None]).astype(jnp.bfloat16)
    row_delta = jnp.sum(grad_low.astype(jnp.float32) * attended_low.astype(jnp.float32), axis=-1)
    piece_rows = every_pair.shape[1]
    key_rows = every_pair[0].reshape(piece_rows, head_count, HD)
    value_rows = every_pair[1].reshape(piece_rows, head_count, HD)
    probability = jnp.exp(scores_of(every_pair[0])) / exp_total[:, :, None]
    prob_grad = jnp.einsum("qhd,khd->hqk", grad_low, value_rows, preferred_element_type=jnp.float32)
    grad_score = (probability * (prob_grad - row_delta.T[:, :, None]) * score_scale).astype(
        jnp.bfloat16
    )
    query_part = jnp.einsum(
        "hqk,khd->qhd", grad_score, key_rows, preferred_element_type=jnp.float32
    )
    key_part = jnp.einsum("hqk,qhd->khd", grad_score, query_low, preferred_element_type=jnp.float32)
    value_part = jnp.einsum(
        "hqk,qhd->khd",
        probability.astype(jnp.bfloat16),
        grad_low,
        preferred_element_type=jnp.float32,
    )
    every_grad = jnp.stack(
        [key_part.reshape(piece_rows, column_count), value_part.reshape(piece_rows, column_count)]
    )
    pair_grad = lax.psum_scatter(
        every_grad.astype(jnp.bfloat16), "seq", scatter_dimension=1, tiled=True
    ).astype(jnp.float32)
    query_back = normalize_back(query_part, query_unit, query_inv)
    key_back = normalize_back(pair_grad[0].reshape(row_count, head_count, HD), key_unit, key_inv)
    qkv_low = jnp.concatenate(
        [
            query_back.reshape(row_count, column_count),
            key_back.reshape(row_count, column_count),
            pair_grad[1],
        ],
        axis=1,
    ).astype(jnp.bfloat16)
    inner_grad = jnp.einsum("rc,dc->rd", qkv_low, full_qkv, preferred_element_type=jnp.float32)
    attended_flat = attended_low.reshape(row_count, column_count)
    share_width = feature_count // lax.axis_size("tensor")
    whole_sum = lax.psum(inner_grad.astype(jnp.bfloat16), "tensor").astype(jnp.float32)
    branch = lax.dynamic_slice_in_dim(
        normalize_back(whole_sum, normed, inverse),
        lax.axis_index("tensor") * share_width,
        share_width,
        1,
    )
    left_rows = unit_low
    right_rows = grad_rows
    qkv_term = jnp.einsum(
        "rd,rc->dc", left_rows, qkv_low, preferred_element_type=jnp.float32
    ).reshape(lax.axis_size(("seq", "dp")) * own_rows, 3, column_count)
    out_term = jnp.einsum(
        "rd,rc->dc", right_rows, attended_flat, preferred_element_type=jnp.float32
    )
    summed = lax.psum_scatter(
        jnp.concatenate([qkv_term, out_term[:, None, :]], axis=1).astype(jnp.bfloat16),
        ("seq", "dp"),
        scatter_dimension=0,
        tiled=True,
    ).astype(jnp.float32)
    return (summed[:, :3], summed[:, 3], branch.astype(jnp.bfloat16)[None])


def solution(mesh):
    return jax.shard_map(
        local,
        mesh=mesh,
        in_specs=(
            P("dp", "seq", None),
            P("dp", "seq", None),
            P(("seq", "dp"), None, "tensor"),
            P(("seq", "dp"), "tensor"),
        ),
        out_specs=(
            P(("seq", "dp"), None, "tensor"),
            P(("seq", "dp"), "tensor"),
            P("dp", "seq", "tensor"),
        ),
        check_vma=False,
    )
```

profile of v0, /device:TPU:0, one launch (start us, length us, event | category | flops | bytes accessed | tf_op | source)
XLA Modules:
  0.0 413.4 jit_solution(1419548005790425770)
XLA Ops:
  7.2 2.0 copy.55
  9.3 0.7 all-gather.8.cloned.1.call-update
  10.0 1.7 convert_reduce_fusion
  11.8 0.6 fusion.6
  12.3 67.3 %all-gather.4.cloned.1.call-done = bf16[3072,1152]{1,0:T(8,128)(2,1)} async-done(((bf16[192,1152]{1,0:T(8,128)(2,1)}), bf16[3072,1152]{1,0:T(8,128)(2,1)}) %all-gather.4.cloned.1.call-update) | async-done | bytes 7077904 | tf_op jit(solution)/shard_map/all_gather | solution.py:36
  79.6 5.3 %fusion.23 = f32[256,1152]{1,0:T(8,128)S(1)} fusion(bf16[3072,1152]{1,0:T(8,128)(2,1)} %all-gather.4.cloned.1.call-done, bf16[1,256,3072]{2,1,0:T(8,128)(2,1)S(1)} %copy-done.1, f32[256]{0:T(256)S(1)} %add_rsqrt_fusion.2, f32[256]{0:T(256)S(1)} %broadcast_multiply_fusion.8), kind=kOutput, calls=%fused_computation.35 | convolution fusion | flops 1815085056 | bytes 9832448 | tf_op jit(solution)/shard_map/dot_general | solution.py:41
  84.9 1.0 copy-done.7
  85.9 0.8 slice.45
  86.7 1.2 copy.27
  87.9 0.1 multiply_reduce_fusion.5
  88.0 0.8 mul.130
  88.8 1.9 copy.29
  90.7 0.8 sub.89
  91.5 1.9 copy.28
  93.5 1.0 fusion.49
  94.5 2.2 fusion.59
  96.7 0.8 pad_maximum_fusion.3
  97.5 25.5 %all-gather.8.cloned.1.call-done = bf16[3072,384]{1,0:T(8,128)(2,1)} async-done(((bf16[192,384]{1,0:T(8,128)(2,1)}), bf16[3072,384]{1,0:T(8,128)(2,1)}) %all-gather.8.cloned.1.call-update) | async-done | bytes 2359312 | tf_op jit(solution)/shard_map/all_gather | solution.py:37
  123.0 2.6 fusion.39
  125.7 0.8 copy.34
  126.5 1.2 copy.31
  127.7 0.1 multiply_reduce_fusion.4
  127.8 33.2 %all-gather.6.cloned.1.call-done = bf16[2,1024,384]{2,1,0:T(8,128)(2,1)} async-done(((bf16[2,256,384]{2,1,0:T(8,128)(2,1)}), bf16[2,1024,384]{2,1,0:T(8,128)(2,1)}) %all-gather.6.cloned.1.call-update) | async-done | bytes 1572880 | tf_op jit(solution)/shard_map/all_gather | solution.py:72
  161.0 2.7 fusion.58
  163.6 2.3 copy.30
  166.0 2.3 copy.35
  168.2 2.0 fusion.9
  170.3 1.7 fusion.27
  171.9 1.3 multiply_reduce_fusion.3
  173.3 1.1 multiply_convert_fusion
  174.4 1.2 copy-done.3
  175.6 1.3 convolution_convert_fusion.3
  176.9 2.3 copy.38
  179.2 2.3 copy.39
  181.5 2.7 pad_maximum_fusion.1
  184.2 0.2 all-reduce.2.cloned.1.call-start
  184.5 2.3 fusion.57
  186.8 0.8 multiply_convert_fusion.1
  187.6 1.7 copy.44
  189.3 29.4 %reduce-scatter.3.cloned.1.call-done = bf16[2,256,384]{2,1,0:T(8,128)(2,1)} async-done(((bf16[2,1024,384]{2,1,0:T(8,128)(2,1)}), bf16[2,256,384]{2,1,0:T(8,128)(2,1)}) %reduce-scatter.3.cloned.1.call-update) | async-done | bytes 393232 | tf_op jit(solution)/shard_map/reduce_scatter | solution.py:106
  218.7 1.9 slice_convert_fusion.1
  220.6 1.9 copy.40
  222.5 1.2 multiply_reduce_fusion.1
  223.7 0.8 mul.146
  224.5 1.9 copy.42
  226.4 0.8 sub.100
  227.2 1.9 copy.41
  229.1 1.6 fusion.46
  230.7 0.7 copy-done.8
  231.4 6.5 %convolution_convert_fusion.2 = bf16[256,3072]{1,0:T(8,128)(2,1)} fusion(bf16[3072,1152]{1,0:T(8,128)(2,1)} %all-gather.4.cloned.1.call-done, bf16[256,384]{1,0:T(8,128)(2,1)S(1)} %copy-done.13, bf16[256,384]{1,0:T(8,128)(2,1)S(1)} %fusion.46, bf16[256,384]{1,0:T(8,128)(2,1)S(1)} %copy-done.10), kind=kOutput, calls=%fused_computation.7 | convolution fusion | flops 1814495232 | bytes 9240576 | tf_op jit(solution)/shard_map/rc,dc->rd/dot_general | solution.py:119
  237.9 0.0 reduce-scatter.5.cloned.1.call-start
  238.0 3.5 fusion
  241.5 0.9 fusion.48
  242.4 2.2 copy.45
  244.5 5.5 %convolution_convert_fusion = bf16[3072,3,384]{2,0,1:T(8,128)(2,1)} fusion(bf16[3,384,256]{2,1,0:T(8,128)(2,1)} %bitcast.107, bf16[1,256,3072]{2,1,0:T(8,128)(2,1)S(1)} %copy-done.1, f32[256]{0:T(256)S(1)} %copy-done.17, f32[256]{0:T(256)S(1)} %copy-done.19), kind=kOutput, calls=%fused_computation.1 | convolution fusion | flops 1818624000 | bytes 9242624 | tf_op jit(solution)/shard_map/rd,rc->dc/dot_general | solution.py:131
  250.1 8.4 %pad_maximum_fusion = bf16[3072,4,384]{2,0,1:T(8,128)(2,1)} fusion(bf16[3072,1,384]{2,0,1:T(8,128)(2,1)} %fusion, bf16[3072,3,384]{2,0,1:T(8,128)(2,1)} %convolution_convert_fusion), kind=kLoop, calls=%fused_computation | loop fusion | flops 4718592 | bytes 18874368 | tf_op jit(solution)/shard_map/concatenate | solution.py:138
  258.5 29.9 %all-reduce.2.cloned.1.call-done = bf16[256,3072]{1,0:T(8,128)(2,1)} async-done(((bf16[256,3072]{1,0:T(8,128)(2,1)}), bf16[256,3072]{1,0:T(8,128)(2,1)}) %all-reduce.2.cloned.1.call-update) | async-done | bytes 1572880 | tf_op jit(solution)/shard_map/psum | solution.py:122
  288.4 1.9 convert_element_type.80
  290.3 1.1 convert_reduce_fusion.1
  291.4 1.2 fusion.43
  292.6 111.0 %reduce-scatter.5.cloned.1.call-done = bf16[192,4,384]{2,0,1:T(8,128)(2,1)} async-done(((bf16[3072,4,384]{2,0,1:T(8,128)(2,1)}), bf16[192,4,384]{2,0,1:T(8,128)(2,1)}) %reduce-scatter.5.cloned.1.call-update) | async-done | bytes 589840 | tf_op jit(solution)/shard_map/reduce_scatter | solution.py:137
  403.6 1.2 convert_element_type.78
  404.9 0.7 slice_bitcast_fusion
  405.6 1.0 slice.52
  (58 shorter events, 0.5 us)
Async XLA Ops:
  7.2 115.9 %copy-start = (bf16[1,256,3072]{2,1,0:T(8,128)(2,1)S(1)}, bf16[1,256,3072]{2,1,0:T(8,128)(2,1)}, u32[]{:S(2)}) copy-start(bf16[1,256,3072]{2,1,0:T(8,128)(2,1)} %param.5) | copy-start | bytes 4718596
  7.2 4.6 %copy-start.1 = (bf16[1,256,3072]{2,1,0:T(8,128)(2,1)S(1)}, bf16[1,256,3072]{2,1,0:T(8,128)(2,1)}, u32[]{:S(2)}) copy-start(bf16[1,256,3072]{2,1,0:T(8,128)(2,1)} %param.4) | copy-start | bytes 4718596
  7.2 72.5 %all-gather.4.cloned.1.call-start = ((), (), s32[]{:S(2)}) async-start(), calls=%async_computation.2 | async-start | bytes 7520256 | tf_op jit(solution)/shard_map/all_gather | solution.py:36
  9.2 113.8 %all-gather.8.cloned.1.call-start = ((), (), s32[]{:S(2)}) async-start(), calls=%async_computation.4 | async-start | bytes 2506752 | tf_op jit(solution)/shard_map/all_gather | solution.py:37
  10.0 151.0 %all-gather.6.cloned.1.call-start = ((), (), s32[]{:S(2)}) async-start(), calls=%async_computation.3 | async-start | bytes 1966080 | tf_op jit(solution)/shard_map/all_gather | solution.py:72
  11.7 73.2 %copy-start.18 = (f32[256]{0:T(256)}, f32[256]{0:T(256)S(1)}, u32[]{:S(2)}) copy-start(f32[256]{0:T(256)S(1)} %broadcast_multiply_fusion.8) | copy-start | bytes 3076
  12.3 72.6 %copy-start.16 = (f32[256]{0:T(256)}, f32[256]{0:T(256)S(1)}, u32[]{:S(2)}) copy-start(f32[256]{0:T(256)S(1)} %add_rsqrt_fusion.2) | copy-start | bytes 3076
  84.9 1.0 copy-start.7
  87.9 8.8 %copy-start.2 = (f32[256,384]{0,1:T(8,128)}, f32[256,384]{0,1:T(8,128)S(1)}, u32[]{:S(2)}) copy-start(f32[256,384]{0,1:T(8,128)S(1)} %copy.27) | copy-start | bytes 1179652
  97.5 121.2 %reduce-scatter.3.cloned.1.call-start = ((), (), s32[]{:S(2)}) async-start(), calls=%async_computation.5 | async-start | bytes 1966080 | tf_op jit(solution)/shard_map/reduce_scatter | solution.py:106
  168.2 2.0 copy-start.15
  170.2 1.7 copy-start.12
  174.4 1.2 copy-start.3
  184.2 104.2 %all-reduce.2.cloned.1.call-start = ((), (), s32[]{:S(2)}) async-start(), calls=%async_computation.7 | async-start | bytes 3145728 | tf_op jit(solution)/shard_map/psum | solution.py:122
  189.3 39.8 %copy-start.6 = (f32[256,384]{1,0:T(8,128)S(1)}, f32[256,384]{1,0:T(8,128)}, u32[]{:S(2)}) copy-start(f32[256,384]{1,0:T(8,128)} %copy.29) | copy-start | bytes 1179652
  229.1 2.3 copy-start.10
  229.1 2.3 copy-start.13
  230.7 0.7 copy-start.8
  237.9 3.6 copy-start.9
  237.9 3.6 copy-start.11
  237.9 165.7 %reduce-scatter.5.cloned.1.call-start = ((), (), s32[]{:S(2)}) async-start(), calls=%async_computation.6 | async-start | bytes 10027008 | tf_op jit(solution)/shard_map/reduce_scatter | solution.py:137
  238.0 3.6 copy-start.14
  238.0 6.6 %copy-start.17 = (f32[256]{0:T(256)S(1)}, f32[256]{0:T(256)}, u32[]{:S(2)}) copy-start(f32[256]{0:T(256)} %copy-done.16) | copy-start | bytes 3076
  238.0 6.6 %copy-start.19 = (f32[256]{0:T(256)S(1)}, f32[256]{0:T(256)}, u32[]{:S(2)}) copy-start(f32[256]{0:T(256)} %copy-done.18) | copy-start | bytes 3076
  288.4 1.9 copy-start.4
  403.6 2.0 copy-start.5
Sparse Core Ops, SparseCore 0:
  10.9 68.7 all-gather.3
  81.9 41.0 all-gather.7
  125.2 35.7 all-gather.5
  184.4 34.2 reduce-scatter.2
  238.0 50.3 all-reduce.1
  292.4 111.2 reduce-scatter.4
where the time goes:
time: 415 us; the launch traced here: 413 us
  waiting for transfers between devices  297 us (72%)
  local copies, waits for them, and re-layouts  40.1 us (10%)
  matrix products  33.2 us (8%)
  other arithmetic  28.3 us (7%)
  between operations  14.4 us (3%)
    reduce_scatter x1, waiting for transfers between devices, local(): lax.psum_scatter(jnp.concatenate([qkv_term, out_term[:, None, :]], axis=1...  111 us
    all_gather x1, waiting for transfers between devices, local(): piece_qkv = lax.all_gather(flat_weight, ('seq', 'dp'), axis=0, tiled=True)  67.3 us
    all_gather x1, waiting for transfers between devices, local(): every_pair = lax.all_gather(key_value, 'seq', axis=1, tiled=True)  33.2 us
    psum x1, waiting for transfers between devices, local(): lax.psum(inner_grad.astype(jnp.bfloat16), 'tensor').astype(jnp.float32)  29.9 us
    reduce_scatter x1, waiting for transfers between devices, local(): lax.psum_scatter(every_grad.astype(jnp.bfloat16), 'seq', scatter_dimensio...  29.4 us
    all_gather x1, waiting for transfers between devices, local(): piece_out = lax.all_gather(out_weight, ('seq', 'dp'), axis=0, tiled=True)  25.5 us
    concatenate x1, other arithmetic, local(): jnp.concatenate([qkv_term, out_term[:, None, :]], axis=1)  8.4 us
  transfers between devices with their start and end apart: 6, of which 6 were waited for; matrix products, arithmetic and copies ran while one was open for 13% of the time, Pallas kernels for 0%

commit v1 on v0

--- a/solution.py
+++ b/solution.py
@@ -1,9 +1,173 @@
+import functools
+
 import jax
 import jax.numpy as jnp
 from jax import lax
+from jax.experimental import pallas as pl
+from jax.experimental.pallas import tpu as pltpu
 from jax.sharding import PartitionSpec as P
 
 HD = 128
+
+CORES = 2
+CHUNKS = 2
+MESH_ID = pl.DeviceIdType.MESH
+
+
+def greet(seq_count, chip_count, place, chip, core):
+    barrier = pltpu.get_barrier_semaphore()
+
+    def signal(device):
+        pl.semaphore_signal(barrier, inc=1, device_id=device, device_id_type=MESH_ID)
+
+    @pl.when(place > 0)
+    def _():
+        signal({"seq": place - 1})
+
+    @pl.when(place < seq_count - 1)
+    def _():
+        signal({"seq": place + 1})
+
+    for step in range(1, chip_count):
+        signal({"dp": (chip + step) % chip_count * CORES + core})
+    signal({"dp": chip * CORES + 1 - core})
+    ends = jnp.minimum(place, 1) + jnp.minimum(seq_count - 1 - place, 1)
+    pl.semaphore_wait(barrier, chip_count + ends)
+
+
+def gather_kernel(
+    seq_count, dp_count, own_ref, out_ref, recv, right_sem, left_sem, chip_sem, core_sem, own_sem
+):
+    chip_count = dp_count // CORES
+    place = lax.axis_index("seq")
+    index = lax.axis_index("dp")
+    chip, core = index // CORES, index % CORES
+    greet(seq_count, chip_count, place, chip, core)
+    own_copy = pltpu.make_async_copy(own_ref, out_ref.at[place * dp_count + index], own_sem)
+    own_copy.start()
+
+    def copy(source, slot, send_sem, device):
+        return pltpu.make_async_remote_copy(
+            src_ref=source,
+            dst_ref=out_ref.at[slot],
+            send_sem=send_sem,
+            recv_sem=recv.at[slot],
+            device_id=device,
+            device_id_type=MESH_ID,
+        )
+
+    def right(source, origin):
+        return copy(
+            source, origin * dp_count + index, right_sem.at[origin], {"seq": place + 1}
+        )
+
+    def left(source, origin):
+        return copy(source, origin * dp_count + index, left_sem.at[origin], {"seq": place - 1})
+
+    def across(source, origin, step):
+        return copy(
+            source,
+            origin * dp_count + index,
+            chip_sem.at[origin * chip_count + step],
+            {"dp": (chip + step) % chip_count * CORES + core},
+        )
+
+    def beside(source, origin, source_chip):
+        return copy(
+            source,
+            origin * dp_count + source_chip * CORES + core,
+            core_sem.at[origin * chip_count + source_chip],
+            {"dp": chip * CORES + 1 - core},
+        )
+
+    def landed(slot):
+        copy(own_ref, slot, core_sem.at[0], {"dp": chip * CORES + 1 - core}).wait_recv()
+
+    def spread(source, origin):
+        for step in range(1, chip_count):
+            across(source, origin, step).start()
+        beside(source, origin, chip).start()
+
+    @pl.when(place < seq_count - 1)
+    def _():
+        right(own_ref, place).start()
+
+    @pl.when(place > 0)
+    def _():
+        left(own_ref, place).start()
+
+    spread(own_ref, place)
+    for step in range(1, seq_count):
+        low, high = place - step, place + step
+
+        @pl.when(low >= 0)
+        def _():
+            slot = low * dp_count + index
+            landed(slot)
+
+            @pl.when(place < seq_count - 1)
+            def _():
+                right(out_ref.at[slot], low).start()
+
+            spread(out_ref.at[slot], low)
+
+        @pl.when(high < seq_count)
+        def _():
+            slot = high * dp_count + index
+            landed(slot)
+
+            @pl.when(place > 0)
+            def _():
+                left(out_ref.at[slot], high).start()
+
+            spread(out_ref.at[slot], high)
+
+    for turn in range(seq_count):
+        origin = (place + turn) % seq_count
+        for step in range(1, chip_count):
+            source_chip = (chip + step) % chip_count
+            slot = origin * dp_count + source_chip * CORES + core
+            landed(slot)
+            beside(out_ref.at[slot], origin, source_chip).start()
+    for origin in range(seq_count):
+        for source_chip in range(chip_count):
+            landed(origin * dp_count + source_chip * CORES + 1 - core)
+    own_copy.wait()
+    for origin in range(seq_count):
+        for step in range(1, chip_count):
+            across(own_ref, origin, step).wait_send()
+        for source_chip in range(chip_count):
+            beside(own_ref, origin, source_chip).wait_send()
+
+        @pl.when((origin <= place) & (place < seq_count - 1))
+        def _():
+            right(own_ref, origin).wait_send()
+
+        @pl.when((origin >= place) & (place > 0))
+        def _():
+            left(own_ref, origin).wait_send()
+
+
+def gather_rows(own):
+    seq_count, dp_count = lax.axis_size("seq"), lax.axis_size("dp")
+    chip_count = dp_count // CORES
+    return pl.pallas_call(
+        functools.partial(gather_kernel, seq_count, dp_count),
+        out_shape=jax.ShapeDtypeStruct((seq_count * dp_count,) + own.shape, own.dtype),
+        in_specs=[pl.BlockSpec(memory_space=pltpu.VMEM)],
+        out_specs=pl.BlockSpec(memory_space=pl.ANY),
+        scratch_shapes=[
+            pltpu.SemaphoreType.DMA((seq_count * dp_count,)),
+            pltpu.SemaphoreType.DMA((seq_count,)),
+            pltpu.SemaphoreType.DMA((seq_count,)),
+            pltpu.SemaphoreType.DMA((seq_count * chip_count,)),
+            pltpu.SemaphoreType.DMA((seq_count * chip_count,)),
+            pltpu.SemaphoreType.DMA,
+        ],
+        compiler_params=pltpu.CompilerParams(collective_id=0, has_side_effects=True),
+        cost_estimate=pl.CostEstimate(flops=0, bytes_accessed=150000000, transcendentals=0),
+        name="gather_rows",
+    )(own)
 
 
 epsilon = 1e-06
@@ -33,8 +197,11 @@
     normed, inverse = normalize(tokens[0].astype(jnp.float32))
     unit_low = normed.astype(jnp.bfloat16)
     flat_weight = qkv_weight.reshape(own_rows, 3 * column_count)
-    piece_qkv = lax.all_gather(flat_weight, ("seq", "dp"), axis=0, tiled=True)
-    piece_out = lax.all_gather(out_weight, ("seq", "dp"), axis=0, tiled=True)
+    piece_all = gather_rows(jnp.concatenate([flat_weight, out_weight], axis=1)).reshape(
+        feature_count, 4 * column_count
+    )
+    piece_qkv = piece_all[:, : 3 * column_count]
+    piece_out = piece_all[:, 3 * column_count :]
     piece_rows = piece_qkv.shape[0]
     left_rows = unit_low
     right_rows = grad_rows

time: 415 us -> 381 us (0.918)
  waiting for transfers between devices: 297 us -> 201 us
  Pallas kernels: 0 us -> 63.2 us
    all_gather x2 -> x0, waiting for transfers between devices: 92.8 us -> none  [the longest x1 67.3 us: local(): piece_qkv = lax.all_gather(flat_weight, ('seq', 'dp'), axis=0, tiled=True)]
    pallas_call x0 -> x1, Pallas kernels: none -> 63.2 us  [gather_rows(): pl.pallas_call(functools.partial(gather_kernel, seq_count, dp_count), out...]
  transfers between devices with their start and end apart: 6 -> 4, of which waited for: 6 -> 4; matrix products, arithmetic and copies ran while one was open for 13% -> 9% of each run, Pallas kernels for 0% -> 0%
where the time goes in v1:
time: 381 us; the launch traced here: 379 us
  waiting for transfers between devices  201 us (53%)
  Pallas kernels  63.2 us (17%)
  local copies, waits for them, and re-layouts  36.4 us (10%)
  matrix products  33.7 us (9%)
  other arithmetic  30.2 us (8%)
  between operations  14.1 us (4%)
    reduce_scatter x1, waiting for transfers between devices, local(): lax.psum_scatter(jnp.concatenate([qkv_term, out_term[:, None, :]], axis=1...  111 us
    pallas_call x1, Pallas kernels, gather_rows(): pl.pallas_call(functools.partial(gather_kernel, seq_count, dp_count), out...  63.2 us
    all_gather x1, waiting for transfers between devices, local(): every_pair = lax.all_gather(key_value, 'seq', axis=1, tiled=True)  31.2 us
    psum x1, waiting for transfers between devices, local(): lax.psum(inner_grad.astype(jnp.bfloat16), 'tensor').astype(jnp.float32)  29.9 us
    reduce_scatter x1, waiting for transfers between devices, local(): lax.psum_scatter(every_grad.astype(jnp.bfloat16), 'seq', scatter_dimensio...  29.4 us
    concatenate x1, other arithmetic, local(): jnp.concatenate([qkv_term, out_term[:, None, :]], axis=1)  8.4 us
  transfers between devices with their start and end apart: 4, of which 4 were waited for; matrix products, arithmetic and copies ran while one was open for 9% of the time, Pallas kernels for 0%

profile of v1, /device:TPU:0, one launch (start us, length us, event | category | flops | bytes accessed | tf_op | source)
XLA Modules:
  0.0 379.5 jit_solution(1550366210741359725)
XLA Ops:
  7.2 0.0 all-gather.2.cloned.1.call-start
  7.3 1.9 convert_reduce_fusion
  9.1 0.2 copy-done.1
  9.3 0.6 fusion.13
  10.0 0.9 pad_maximum_fusion.2.own_ref
  10.8 63.2 %gather_rows.1 = bf16[16,192,1536]{2,1,0:T(8,128)(2,1)} custom-call(bf16[192,1536]{1,0:T(8,128)(2,1)} %pad_maximum_fusion.2.own_ref), custom_call_target="tpu_custom_call" | custom-call | bytes 150000000 | tf_op jit(solution)/shard_map/gather_rows/pallas_call | solution.py:154
  74.0 5.3 %fusion.2 = f32[256,1152]{1,0:T(8,128)S(1)} fusion(bf16[3072,1536]{1,0:T(8,128)(2,1)} %bitcast.101, bf16[1,256,3072]{2,1,0:T(8,128)(2,1)S(1)} %copy-done.1, f32[256]{0:T(256)S(1)} %add_rsqrt_fusion.2, f32[256]{0:T(256)S(1)} %broadcast_multiply_fusion.8), kind=kOutput, calls=%fused_computation.3 | convolution fusion | flops 1815085056 | bytes 9832448 | tf_op jit(solution)/shard_map/dot_general | solution.py:208
  79.3 0.8 fusion.58
  80.1 0.4 copy-done.7
  80.4 0.8 slice.54
  81.2 1.2 copy.26
  82.4 0.1 multiply_reduce_fusion.5
  82.5 0.8 mul.130
  83.3 1.9 copy.28
  85.2 0.8 sub.89
  86.0 1.9 copy.27
  87.9 2.2 fusion.68
  90.1 1.7 pad_maximum_fusion.4
  91.8 0.0 reduce-scatter.3.cloned.1.call-start
  91.9 1.2 copy.30
  93.1 0.1 multiply_reduce_fusion.4
  93.2 3.2 fusion.46
  96.3 31.2 %all-gather.2.cloned.1.call-done = bf16[2,1024,384]{2,1,0:T(8,128)(2,1)} async-done(((bf16[2,256,384]{2,1,0:T(8,128)(2,1)}), bf16[2,1024,384]{2,1,0:T(8,128)(2,1)}) %all-gather.2.cloned.1.call-update) | async-done | bytes 1572880 | tf_op jit(solution)/shard_map/all_gather | solution.py:239
  127.5 2.7 fusion.67
  130.2 2.3 copy.29
  132.5 2.3 copy.33
  134.7 2.0 fusion.16
  136.8 1.7 fusion.34
  138.4 1.3 multiply_reduce_fusion.3
  139.8 1.1 multiply_convert_fusion
  140.9 1.1 copy-done.3
  142.1 1.3 convolution_convert_fusion.2
  143.3 2.3 copy.36
  145.6 2.3 copy.37
  147.9 2.7 pad_maximum_fusion.1
  150.7 0.2 all-reduce.2.cloned.1.call-start
  150.9 2.3 fusion.66
  153.2 0.8 multiply_convert_fusion.1
  154.0 1.7 copy.42
  155.8 29.4 %reduce-scatter.3.cloned.1.call-done = bf16[2,256,384]{2,1,0:T(8,128)(2,1)} async-done(((bf16[2,1024,384]{2,1,0:T(8,128)(2,1)}), bf16[2,256,384]{2,1,0:T(8,128)(2,1)}) %reduce-scatter.3.cloned.1.call-update) | async-done | bytes 393232 | tf_op jit(solution)/shard_map/reduce_scatter | solution.py:273
  185.1 1.9 slice_convert_fusion.1
  187.0 1.9 copy.38
  188.9 1.2 multiply_reduce_fusion.1
  190.1 0.8 mul.146
  190.9 1.9 copy.40
  192.8 0.8 sub.100
  193.6 1.9 copy.39
  195.5 1.6 fusion.55
  197.1 0.7 copy-done.8
  197.8 6.5 %fusion.5 = bf16[256,3072]{1,0:T(8,128)(2,1)} fusion(bf16[3072,1536]{1,0:T(8,128)(2,1)} %bitcast.103, bf16[256,384]{1,0:T(8,128)(2,1)S(1)} %copy-done.13, bf16[256,384]{1,0:T(8,128)(2,1)S(1)} %fusion.55, bf16[256,384]{1,0:T(8,128)(2,1)S(1)} %copy-done.10), kind=kOutput, calls=%fused_computation.11 | convolution fusion | flops 1814495232 | bytes 9240576 | tf_op jit(solution)/shard_map/rc,dc->rd/dot_general | solution.py:286
  204.3 0.0 reduce-scatter.5.cloned.1.call-start
  204.4 3.5 fusion.4
  207.9 0.9 fusion.57
  208.8 2.1 copy.43
  210.9 5.5 %convolution_convert_fusion = bf16[3072,3,384]{2,0,1:T(8,128)(2,1)} fusion(bf16[3,384,256]{2,1,0:T(8,128)(2,1)} %bitcast.110, bf16[1,256,3072]{2,1,0:T(8,128)(2,1)S(1)} %copy-done.1, f32[256]{0:T(256)S(1)} %copy-done.18, f32[256]{0:T(256)S(1)} %copy-done.20), kind=kOutput, calls=%fused_computation.5 | convolution fusion | flops 1818624000 | bytes 9242624 | tf_op jit(solution)/shard_map/rd,rc->dc/dot_general | solution.py:298
  216.5 8.4 %pad_maximum_fusion = bf16[3072,4,384]{2,0,1:T(8,128)(2,1)} fusion(bf16[3072,1,384]{2,0,1:T(8,128)(2,1)} %fusion.4, bf16[3072,3,384]{2,0,1:T(8,128)(2,1)} %convolution_convert_fusion), kind=kLoop, calls=%fused_computation | loop fusion | flops 4718592 | bytes 18874368 | tf_op jit(solution)/shard_map/concatenate | solution.py:305
  224.9 29.9 %all-reduce.2.cloned.1.call-done = bf16[256,3072]{1,0:T(8,128)(2,1)} async-done(((bf16[256,3072]{1,0:T(8,128)(2,1)}), bf16[256,3072]{1,0:T(8,128)(2,1)}) %all-reduce.2.cloned.1.call-update) | async-done | bytes 1572880 | tf_op jit(solution)/shard_map/psum | solution.py:289
  254.8 1.9 convert_element_type.84
  256.7 1.1 convert_reduce_fusion.1
  257.8 1.2 fusion.52
  259.0 111.0 %reduce-scatter.5.cloned.1.call-done = bf16[192,4,384]{2,0,1:T(8,128)(2,1)} async-done(((bf16[3072,4,384]{2,0,1:T(8,128)(2,1)}), bf16[192,4,384]{2,0,1:T(8,128)(2,1)}) %reduce-scatter.5.cloned.1.call-update) | async-done | bytes 589840 | tf_op jit(solution)/shard_map/reduce_scatter | solution.py:304
  370.0 1.2 convert_element_type.82
  371.2 0.7 slice_bitcast_fusion
  372.0 1.0 slice.62
  (57 shorter events, 0.3 us)
Async XLA Ops:
  7.2 86.0 %copy-start = (bf16[1,256,3072]{2,1,0:T(8,128)(2,1)S(1)}, bf16[1,256,3072]{2,1,0:T(8,128)(2,1)}, u32[]{:S(2)}) copy-start(bf16[1,256,3072]{2,1,0:T(8,128)(2,1)} %param.5) | copy-start | bytes 4718596
  7.2 2.1 copy-start.1
  7.2 2.8 copy-start.16
  7.2 120.3 %all-gather.2.cloned.1.call-start = ((), (), s32[]{:S(2)}) async-start(), calls=%async_computation.2 | async-start | bytes 1966080 | tf_op jit(solution)/shard_map/all_gather | solution.py:239
  7.2 2.6 copy-start.15
  9.3 64.7 %copy-start.19 = (f32[256]{0:T(256)}, f32[256]{0:T(256)S(1)}, u32[]{:S(2)}) copy-start(f32[256]{0:T(256)S(1)} %broadcast_multiply_fusion.8) | copy-start | bytes 3076
  9.9 64.1 %copy-start.17 = (f32[256]{0:T(256)}, f32[256]{0:T(256)S(1)}, u32[]{:S(2)}) copy-start(f32[256]{0:T(256)S(1)} %add_rsqrt_fusion.2) | copy-start | bytes 3076
  79.3 1.1 copy-start.7
  82.4 7.7 %copy-start.2 = (f32[256,384]{0,1:T(8,128)}, f32[256,384]{0,1:T(8,128)S(1)}, u32[]{:S(2)}) copy-start(f32[256,384]{0,1:T(8,128)S(1)} %copy.26) | copy-start | bytes 1179652
  91.8 93.3 %reduce-scatter.3.cloned.1.call-start = ((), (), s32[]{:S(2)}) async-start(), calls=%async_computation.3 | async-start | bytes 1966080 | tf_op jit(solution)/shard_map/reduce_scatter | solution.py:273
  134.7 2.0 copy-start.21
  136.7 1.7 copy-start.12
  140.9 1.1 copy-start.3
  150.7 104.1 %all-reduce.2.cloned.1.call-start = ((), (), s32[]{:S(2)}) async-start(), calls=%async_computation.5 | async-start | bytes 3145728 | tf_op jit(solution)/shard_map/psum | solution.py:289
  155.8 39.7 %copy-start.6 = (f32[256,384]{1,0:T(8,128)S(1)}, f32[256,384]{1,0:T(8,128)}, u32[]{:S(2)}) copy-start(f32[256,384]{1,0:T(8,128)} %copy.28) | copy-start | bytes 1179652
  195.5 2.3 copy-start.10
  195.5 2.3 copy-start.13
  197.1 0.7 copy-start.8
  204.3 3.6 copy-start.9
  204.3 3.6 copy-start.11
  204.3 165.7 %reduce-scatter.5.cloned.1.call-start = ((), (), s32[]{:S(2)}) async-start(), calls=%async_computation.4 | async-start | bytes 10027008 | tf_op jit(solution)/shard_map/reduce_scatter | solution.py:304
  204.4 3.6 copy-start.14
  204.4 6.6 %copy-start.18 = (f32[256]{0:T(256)S(1)}, f32[256]{0:T(256)}, u32[]{:S(2)}) copy-start(f32[256]{0:T(256)} %copy-done.17) | copy-start | bytes 3076
  204.4 6.6 %copy-start.20 = (f32[256]{0:T(256)S(1)}, f32[256]{0:T(256)}, u32[]{:S(2)}) copy-start(f32[256]{0:T(256)} %copy-done.19) | copy-start | bytes 3076
  254.8 1.9 copy-start.4
  370.0 2.0 copy-start.5
Sparse Core Ops, SparseCore 0:
  91.9 35.5 all-gather.1
  150.8 34.2 reduce-scatter.2
  204.4 50.3 all-reduce.1
  258.8 111.2 reduce-scatter.4

commit v2 on v1

--- a/solution.py
+++ b/solution.py
@@ -169,6 +169,181 @@
         name="gather_rows",
     )(own)
 
+def scatter_kernel(
+    seq_count,
+    dp_count,
+    term_ref,
+    out_ref,
+    held,
+    chip_in,
+    low_in,
+    high_in,
+    core_recv,
+    core_send,
+    chip_recv,
+    chip_send,
+    low_recv,
+    high_recv,
+    chain_send,
+):
+    chip_count = dp_count // CORES
+    part_rows = term_ref.shape[1] // CHUNKS
+    place = lax.axis_index("seq")
+    index = lax.axis_index("dp")
+    chip, core = index // CORES, index % CORES
+    greet(seq_count, chip_count, place, chip, core)
+
+    def piece(ref, slot, part):
+        return ref.at[slot, pl.ds(part * part_rows, part_rows)]
+
+    def copy(source, target_ref, part, slot, send_sem, recv_sem, device):
+        return pltpu.make_async_remote_copy(
+            src_ref=source,
+            dst_ref=piece(target_ref, slot, part),
+            send_sem=send_sem.at[slot * CHUNKS + part],
+            recv_sem=recv_sem.at[slot * CHUNKS + part],
+            device_id=device,
+            device_id_type=MESH_ID,
+        )
+
+    def beside(part, target, target_chip):
+        source = piece(term_ref, target * dp_count + target_chip * CORES + 1 - core, part)
+        slot = target * chip_count + target_chip
+        device = {"dp": chip * CORES + 1 - core}
+        return copy(source, held, part, slot, core_send, core_recv, device)
+
+    def across(part, target, step):
+        other = (chip + step) % chip_count
+        source = piece(held, target * chip_count + other, part)
+        slot = (step - 1) * seq_count + target
+        device = {"dp": other * CORES + core}
+        return copy(source, chip_in, part, slot, chip_send, chip_recv, device)
+
+    def upward(part, target):
+        source = piece(held, target * chip_count + chip, part)
+        return copy(source, low_in, part, target, chain_send, low_recv, {"seq": place + 1})
+
+    def downward(part, target):
+        source = piece(held, target * chip_count + chip, part)
+        return copy(source, high_in, part, target, chain_send, high_recv, {"seq": place - 1})
+
+    def add(slot, part, others):
+        @pl.loop(0, part_rows // 16)
+        def _(step):
+            rows = pl.ds(pl.multiple_of(part * part_rows + step * 16, 16), 16)
+            total = held[slot, rows, :].astype(jnp.float32)
+            for ref, other in others:
+                total = total + ref[other, rows, :].astype(jnp.float32)
+            held[slot, rows, :] = total.astype(held.dtype)
+
+    order = []
+    for turn in range((seq_count + 1) // 2):
+        order.extend(sorted({seq_count - 1 - turn, turn}, reverse=True))
+    items = [(part, target) for part in range(CHUNKS) for target in order]
+    for part, target in items:
+        for step in range(1, chip_count):
+            beside(part, target, (chip + step) % chip_count).start()
+    for part, target in items:
+        beside(part, target, chip).start()
+    for part, target in items:
+        for step in range(1, chip_count):
+            other = (chip + step) % chip_count
+            beside(part, target, other).wait_recv()
+            own_slot = target * dp_count + other * CORES + core
+            add(target * chip_count + other, part, [(term_ref, own_slot)])
+            across(part, target, step).start()
+    for part, target in items:
+        slot = target * chip_count + chip
+        others = [(term_ref, target * dp_count + index)]
+        beside(part, target, chip).wait_recv()
+        for step in range(1, chip_count):
+            across(part, target, step).wait_recv()
+            others.append((chip_in, (step - 1) * seq_count + target))
+        add(slot, part, others)
+        if target > 0:
+
+            @pl.when(place < target)
+            def _():
+                @pl.when(place > 0)
+                def _():
+                    upward(part, target).wait_recv()
+                    add(slot, part, [(low_in, target)])
+
+                upward(part, target).start()
+
+        if target < seq_count - 1:
+
+            @pl.when(place > target)
+            def _():
+                @pl.when(place < seq_count - 1)
+                def _():
+                    downward(part, target).wait_recv()
+                    add(slot, part, [(high_in, target)])
+
+                downward(part, target).start()
+
+    out_ref[...] = held[place * chip_count + chip].astype(jnp.float32)
+
+    @pl.when(place > 0)
+    def _():
+        for part in range(CHUNKS):
+            upward(part, place).wait_recv()
+        out_ref[...] += low_in[place].astype(jnp.float32)
+
+    @pl.when(place < seq_count - 1)
+    def _():
+        for part in range(CHUNKS):
+            downward(part, place).wait_recv()
+        out_ref[...] += high_in[place].astype(jnp.float32)
+
+    for part, target in items:
+        for step in range(1, chip_count):
+            across(part, target, step).wait_send()
+        for target_chip in range(chip_count):
+            beside(part, target, target_chip).wait_send()
+
+        @pl.when(place != target)
+        def _():
+            upward(part, target).wait_send()
+
+
+def scatter_rows(terms):
+    seq_count, dp_count = lax.axis_size("seq"), lax.axis_size("dp")
+    chip_count = dp_count // CORES
+    shape = terms.shape[1:]
+
+    def slots(count):
+        return pltpu.VMEM((count,) + shape, terms.dtype)
+
+    def semaphores(count):
+        return pltpu.SemaphoreType.DMA((count * CHUNKS,))
+
+    both, peers = seq_count * chip_count, seq_count * (chip_count - 1)
+    return pl.pallas_call(
+        functools.partial(scatter_kernel, seq_count, dp_count),
+        out_shape=jax.ShapeDtypeStruct(shape, jnp.float32),
+        in_specs=[pl.BlockSpec(memory_space=pltpu.VMEM)],
+        out_specs=pl.BlockSpec(memory_space=pltpu.VMEM),
+        scratch_shapes=[
+            slots(both),
+            slots(peers),
+            slots(seq_count),
+            slots(seq_count),
+            semaphores(both),
+            semaphores(both),
+            semaphores(peers),
+            semaphores(peers),
+            semaphores(seq_count),
+            semaphores(seq_count),
+            semaphores(seq_count),
+        ],
+        compiler_params=pltpu.CompilerParams(
+            collective_id=1, has_side_effects=True, vmem_limit_bytes=40 * 1024 * 1024
+        ),
+        cost_estimate=pl.CostEstimate(flops=0, bytes_accessed=180000000, transcendentals=0),
+        name="scatter_rows",
+    )(terms)
+
 
 epsilon = 1e-06
 
@@ -286,28 +461,43 @@
     inner_grad = jnp.einsum("rc,dc->rd", qkv_low, full_qkv, preferred_element_type=jnp.float32)
     attended_flat = attended_low.reshape(row_count, column_count)
     share_width = feature_count // lax.axis_size("tensor")
-    whole_sum = lax.psum(inner_grad.astype(jnp.bfloat16), "tensor").astype(jnp.float32)
-    branch = lax.dynamic_slice_in_dim(
-        normalize_back(whole_sum, normed, inverse),
-        lax.axis_index("tensor") * share_width,
-        share_width,
-        1,
-    )
+    tensor_count, tensor_at = lax.axis_size("tensor"), lax.axis_index("tensor")
+
+    def share_of(values, owner):
+        return lax.dynamic_slice_in_dim(values, owner * share_width, share_width, 1)
+
+    def shifted(values, step):
+        pairs = [(place, (place + step) % tensor_count) for place in range(tensor_count)]
+        return lax.ppermute(values, "tensor", pairs)
+
+    inner_low = inner_grad.astype(jnp.bfloat16)
+    share = share_of(inner_low, tensor_at).astype(jnp.float32)
+    for step in range(1, tensor_count):
+        sent = share_of(inner_low, (tensor_at + step) % tensor_count)
+        share = share + shifted(sent, step).astype(jnp.float32)
+    unit_share = share_of(normed, tensor_at)
+    own_sums = jnp.stack([jnp.sum(share, axis=-1), jnp.sum(share * unit_share, axis=-1)])
+    both_sums = own_sums
+    for step in range(1, tensor_count):
+        both_sums = both_sums + shifted(own_sums, step)
+    means = both_sums[:, :, None] / feature_count
+    branch = (share - means[0] - unit_share * means[1]) * inverse
     left_rows = unit_low
     right_rows = grad_rows
     qkv_term = jnp.einsum(
         "rd,rc->dc", left_rows, qkv_low, preferred_element_type=jnp.float32
-    ).reshape(lax.axis_size(("seq", "dp")) * own_rows, 3, column_count)
+    ).astype(jnp.bfloat16)
     out_term = jnp.einsum(
         "rd,rc->dc", right_rows, attended_flat, preferred_element_type=jnp.float32
-    )
-    summed = lax.psum_scatter(
-        jnp.concatenate([qkv_term, out_term[:, None, :]], axis=1).astype(jnp.bfloat16),
-        ("seq", "dp"),
-        scatter_dimension=0,
-        tiled=True,
-    ).astype(jnp.float32)
-    return (summed[:, :3], summed[:, 3], branch.astype(jnp.bfloat16)[None])
+    ).astype(jnp.bfloat16)
+    summed = scatter_rows(
+        jnp.concatenate([qkv_term, out_term], axis=1).reshape(-1, own_rows, 4 * column_count)
+    )
+    return (
+        summed[:, : 3 * column_count].reshape(own_rows, 3, column_count),
+        summed[:, 3 * column_count :],
+        branch.astype(jnp.bfloat16)[None],
+    )
 
 
 def solution(mesh):

time: 381 us -> 337 us (0.88); the launches traced: 379 us -> 331 us
  waiting for transfers between devices: 201 us -> 72.5 us
  Pallas kernels: 63.2 us -> 130 us
  local copies, waits for them, and re-layouts: 36.4 us -> 53 us
  matrix products: 33.7 us -> 26.7 us
    reduce_scatter x1 -> x0, waiting for transfers between devices: 111 us -> none  [local(): lax.psum_scatter(jnp.concatenate([qkv_term, out_term[:, None, :]], axis=1...]
    pallas_call x0 -> x1, Pallas kernels: none -> 66.5 us  [scatter_rows(): pl.pallas_call(functools.partial(scatter_kernel, seq_count, dp_count), ou...]
    psum x1 -> x0, waiting for transfers between devices: 29.9 us -> none  [local(): lax.psum(inner_grad.astype(jnp.bfloat16), 'tensor').astype(jnp.float32)]
    concatenate x0 -> x1, local copies, waits for them, and re-layouts: none -> 12.7 us  [local(): jnp.concatenate([qkv_term, out_term], axis=1)]
    ppermute x0 -> x2, waiting for transfers between devices: none -> 11.9 us  [shifted(): return lax.ppermute(values, 'tensor', pairs)]
    unnamed x44 -> x54, local copies, waits for them, and re-layouts: 2.44 us -> 7.47 us
  transfers between devices with their start and end apart: 4 -> 4, of which waited for: 4 -> 3; matrix products, arithmetic and copies ran while one was open for 9% -> 12% of each run, Pallas kernels for 0% -> 20%
where the time goes in v2:
time: 337 us; the launch traced here: 331 us
  Pallas kernels  130 us (39%)
  waiting for transfers between devices  72.5 us (22%)
  local copies, waits for them, and re-layouts  53 us (16%)
  other arithmetic  31.8 us (9%)
  matrix products  26.7 us (8%)
  between operations  14.4 us (4%)
    pallas_call x1, Pallas kernels, scatter_rows(): pl.pallas_call(functools.partial(scatter_kernel, seq_count, dp_count), ou...  66.5 us
    pallas_call x1, Pallas kernels, gather_rows(): pl.pallas_call(functools.partial(gather_kernel, seq_count, dp_count), out...  63.2 us
    all_gather x1, waiting for transfers between devices, local(): every_pair = lax.all_gather(key_value, 'seq', axis=1, tiled=True)  31 us
    reduce_scatter x1, waiting for transfers between devices, local(): lax.psum_scatter(every_grad.astype(jnp.bfloat16), 'seq', scatter_dimensio...  29.6 us
    concatenate x1, local copies, waits for them, and re-layouts, local(): jnp.concatenate([qkv_term, out_term], axis=1)  12.7 us
    ppermute x2, waiting for transfers between devices, shifted(): return lax.ppermute(values, 'tensor', pairs)  11.9 us
    concatenate x1, other arithmetic, local(): jnp.concatenate([qkv_term, out_term], axis=1)  9.9 us
    unnamed x54, local copies, waits for them, and re-layouts  7.47 us
  transfers between devices with their start and end apart: 4, of which 3 were waited for; matrix products, arithmetic and copies ran while one was open for 12% of the time, Pallas kernels for 20%

profile of v2, /device:TPU:0, one launch (start us, length us, event | category | flops | bytes accessed | tf_op | source)
XLA Modules:
  0.0 331.4 jit_solution(17529133799963438063)
XLA Ops:
  7.3 1.9 convert_reduce_fusion
  9.1 0.2 copy-done.2
  9.3 0.6 fusion.11
  10.0 0.9 pad_maximum_fusion.2.own_ref
  10.8 63.2 %gather_rows.1 = bf16[16,192,1536]{2,1,0:T(8,128)(2,1)} custom-call(bf16[192,1536]{1,0:T(8,128)(2,1)} %pad_maximum_fusion.2.own_ref), custom_call_target="tpu_custom_call" | custom-call | bytes 150000000 | tf_op jit(solution)/shard_map/gather_rows/pallas_call | solution.py:154
  74.0 5.3 %fusion.2 = f32[256,1152]{1,0:T(8,128)S(1)} fusion(bf16[3072,1536]{1,0:T(8,128)(2,1)} %bitcast.99, bf16[1,256,3072]{2,1,0:T(8,128)(2,1)S(1)} %copy-done.2, f32[256]{0:T(256)S(1)} %add_rsqrt_fusion.2, f32[256]{0:T(256)S(1)} %broadcast_multiply_fusion.6), kind=kOutput, calls=%fused_computation.4 | convolution fusion | flops 1815085056 | bytes 9832448 | tf_op jit(solution)/shard_map/dot_general | solution.py:383
  79.3 0.8 slice.64
  80.1 0.4 copy-done.11
  80.5 0.7 fusion.50
  81.2 1.2 copy.25
  82.5 0.8 mul.131
  83.3 1.9 copy.27
  85.2 0.8 sub.84
  86.0 1.9 copy.26
  87.9 2.2 fusion.62
  90.1 1.7 pad_maximum_fusion.4
  91.8 0.2 reduce-scatter.2.cloned.1.call-start
  92.0 1.2 copy.29
  93.3 3.2 fusion.37
  96.5 31.0 %all-gather.2.cloned.1.call-done = bf16[2,1024,384]{2,1,0:T(8,128)(2,1)} async-done(((bf16[2,256,384]{2,1,0:T(8,128)(2,1)}), bf16[2,1024,384]{2,1,0:T(8,128)(2,1)}) %all-gather.2.cloned.1.call-update) | async-done | bytes 1572880 | tf_op jit(solution)/shard_map/all_gather | solution.py:414
  127.5 2.7 fusion.61
  130.1 2.3 copy.28
  132.4 2.3 copy.32
  134.7 2.0 fusion.14
  136.7 1.7 fusion.24
  138.4 1.3 multiply_reduce_fusion.3
  139.8 1.1 multiply_convert_fusion
  140.9 1.1 copy-done.6
  142.0 1.3 convolution_convert_fusion.2
  143.3 2.3 copy.35
  145.6 2.3 copy.36
  147.9 2.7 pad_maximum_fusion.1
  150.7 2.3 fusion.60
  153.0 0.8 multiply_convert_fusion.2
  153.8 1.7 copy.41
  155.5 29.6 %reduce-scatter.2.cloned.1.call-done = bf16[2,256,384]{2,1,0:T(8,128)(2,1)} async-done(((bf16[2,1024,384]{2,1,0:T(8,128)(2,1)}), bf16[2,256,384]{2,1,0:T(8,128)(2,1)}) %reduce-scatter.2.cloned.1.call-update) | async-done | bytes 393232 | tf_op jit(solution)/shard_map/reduce_scatter | solution.py:448
  185.1 1.9 slice_convert_fusion.1
  187.0 1.9 copy.37
  188.9 1.2 multiply_reduce_fusion.1
  190.1 0.8 sub.95
  190.9 1.9 copy.38
  192.8 0.8 mul.147
  193.6 1.9 copy.39
  195.5 1.6 fusion.48
  197.2 5.4 %fusion.5 = bf16[256,3072]{1,0:T(8,128)(2,1)S(1)} fusion(bf16[3072,1536]{1,0:T(8,128)(2,1)} %bitcast.101, bf16[256,384]{1,0:T(8,128)(2,1)S(1)} %copy-done.17, bf16[256,384]{1,0:T(8,128)(2,1)S(1)} %fusion.48, bf16[256,384]{1,0:T(8,128)(2,1)S(1)} %copy-done.15), kind=kOutput, calls=%fused_computation.10 | convolution fusion | flops 1814495232 | bytes 9240576 | tf_op jit(solution)/shard_map/rc,dc->rd/dot_general | solution.py:461
  202.5 1.2 copy-done.7
  203.7 0.9 constant_dynamic-slice_fusion
  204.7 1.5 collective-permute-start
  206.1 2.3 fusion.9
  208.4 0.8 fusion.4
  209.2 0.1 copy-done.14
  209.4 0.1 copy-done.18
  209.5 2.4 convolution_convert_fusion
  212.0 11.9 %collective-permute-done = bf16[256,1536]{1,0:T(8,128)(2,1)} collective-permute-done((bf16[256,1536]{1,0:T(8,128)(2,1)}, bf16[256,1536]{1,0:T(8,128)(2,1)}, u32[]{:S(2)}, u32[]{:S(2)}) %collective-permute-start) | collective-permute-done | bytes 786464 | tf_op jit(solution)/shard_map/ppermute | solution.py:471
  223.9 1.6 fusion.27
  225.5 1.6 collective-permute-start.1
  227.0 9.9 %pad_maximum_fusion = bf16[3072,1536]{0,1:T(8,128)(2,1)} fusion(bf16[3072,384]{0,1:T(8,128)(2,1)S(1)} %fusion.4, bf16[3072,1152]{0,1:T(8,128)(2,1)S(1)} %convolution_convert_fusion), kind=kLoop, calls=%fused_computation.1 | loop fusion | flops 18874368 | bytes 18874368 | tf_op jit(solution)/shard_map/concatenate | solution.py:494
  236.9 12.7 %copy.42 = bf16[3072,1536]{1,0:T(8,128)(2,1)} copy(bf16[3072,1536]{0,1:T(8,128)(2,1)} %pad_maximum_fusion) | data formatting | bytes 18874368 | tf_op jit(solution)/shard_map/concatenate | solution.py:494
  249.6 3.7 %copy-done.1 = bf16[3072,1536]{1,0:T(8,128)(2,1)S(1)} copy-done((bf16[3072,1536]{1,0:T(8,128)(2,1)S(1)}, bf16[3072,1536]{1,0:T(8,128)(2,1)}, u32[]{:S(2)}) %copy-start.1) | copy-done | bytes 9437208
  253.3 66.5 %scatter_rows.1 = f32[192,1536]{1,0:T(8,128)S(1)} custom-call(bf16[16,192,1536]{2,1,0:T(8,128)(2,1)S(1)} %bitcast.92), custom_call_target="tpu_custom_call" | custom-call | bytes 180000000 | tf_op jit(solution)/shard_map/scatter_rows/pallas_call | solution.py:322
  319.9 0.7 slice.60
  320.6 1.0 copy.51
  321.6 0.5 copy-done.4
  322.1 2.4 fusion.43
  (67 shorter events, 0.6 us)
Async XLA Ops:
  7.2 86.2 %copy-start = (bf16[1,256,3072]{2,1,0:T(8,128)(2,1)S(1)}, bf16[1,256,3072]{2,1,0:T(8,128)(2,1)}, u32[]{:S(2)}) copy-start(bf16[1,256,3072]{2,1,0:T(8,128)(2,1)} %param.5) | copy-start | bytes 4718596
  7.2 2.1 copy-start.2
  7.2 2.8 copy-start.21
  7.2 120.3 %all-gather.2.cloned.1.call-start = ((), (), s32[]{:S(2)}) async-start(), calls=%async_computation.1 | async-start | bytes 1966080 | tf_op jit(solution)/shard_map/all_gather | solution.py:414
  7.2 2.6 copy-start.19
  9.3 64.7 %copy-start.24 = (f32[256]{0:T(256)}, f32[256]{0:T(256)S(1)}, u32[]{:S(2)}) copy-start(f32[256]{0:T(256)S(1)} %broadcast_multiply_fusion.6) | copy-start | bytes 3076
  9.9 64.1 %copy-start.22 = (f32[256]{0:T(256)}, f32[256]{0:T(256)S(1)}, u32[]{:S(2)}) copy-start(f32[256]{0:T(256)S(1)} %add_rsqrt_fusion.2) | copy-start | bytes 3076
  79.3 1.2 copy-start.11
  82.4 7.7 %copy-start.5 = (f32[256,384]{0,1:T(8,128)}, f32[256,384]{0,1:T(8,128)S(1)}, u32[]{:S(2)}) copy-start(f32[256,384]{0,1:T(8,128)S(1)} %copy.25) | copy-start | bytes 1179652
  91.8 93.3 %reduce-scatter.2.cloned.1.call-start = ((), (), s32[]{:S(2)}) async-start(), calls=%async_computation.2 | async-start | bytes 1966080 | tf_op jit(solution)/shard_map/reduce_scatter | solution.py:448
  134.7 2.0 copy-start.26
  136.7 1.7 copy-start.12
  140.9 1.1 copy-start.6
  155.5 40.0 %copy-start.10 = (f32[256,384]{1,0:T(8,128)S(1)}, f32[256,384]{1,0:T(8,128)}, u32[]{:S(2)}) copy-start(f32[256,384]{1,0:T(8,128)} %copy.27) | copy-start | bytes 1179652
  195.5 1.6 copy-start.15
  195.5 1.6 copy-start.17
  197.1 5.4 %copy-start.13 = (bf16[256,384]{1,0:T(8,128)(2,1)}, bf16[256,384]{1,0:T(8,128)(2,1)S(1)}, u32[]{:S(2)}) copy-start(bf16[256,384]{1,0:T(8,128)(2,1)S(1)} %fusion.48) | copy-start | bytes 589828
  197.1 9.0 %copy-start.23 = (f32[256]{0:T(256)S(1)}, f32[256]{0:T(256)}, u32[]{:S(2)}) copy-start(f32[256]{0:T(256)} %copy-done.22) | copy-start | bytes 3076
  197.1 9.0 %copy-start.25 = (f32[256]{0:T(256)S(1)}, f32[256]{0:T(256)}, u32[]{:S(2)}) copy-start(f32[256]{0:T(256)} %copy-done.24) | copy-start | bytes 3076
  202.5 1.2 copy-start.7
  204.7 3.8 %copy-start.20 = (bf16[256,3,128]{0,2,1:T(8,128)(2,1)S(1)}, bf16[256,3,128]{0,2,1:T(8,128)(2,1)}, u32[]{:S(2)}) copy-start(bf16[256,3,128]{0,2,1:T(8,128)(2,1)} %get-tuple-element.26) | copy-start | bytes 589828
  204.7 19.2 %collective-permute-start = (bf16[256,1536]{1,0:T(8,128)(2,1)}, bf16[256,1536]{1,0:T(8,128)(2,1)}, u32[]{:S(2)}, u32[]{:S(2)}) collective-permute-start(bf16[256,1536]{1,0:T(8,128)(2,1)} %constant_dynamic-slice_fusion), channel_id=1, source_target_pairs={{0,4},{4,0},{1,5},{5,1},{2,6},{6,2},{3,7},{7,3},{8,12},{12,8},{9,1... | collective-permute-start | bytes 2359304 | tf_op jit(solution)/shard_map/ppermute | solution.py:471
  208.4 0.9 copy-start.14
  208.4 1.0 copy-start.16
  208.4 1.1 copy-start.18
  209.5 14.3 %copy-start.3 = (f32[256,3072]{1,0:T(8,128)S(1)}, f32[256,3072]{1,0:T(8,128)}, u32[]{:S(2)}) copy-start(f32[256,3072]{1,0:T(8,128)} %fusion.9) | copy-start | bytes 9437188
  209.5 14.3 %copy-start.8 = (bf16[256,3072]{1,0:T(8,128)(2,1)S(1)}, bf16[256,3072]{1,0:T(8,128)(2,1)}, u32[]{:S(2)}) copy-start(bf16[256,3072]{1,0:T(8,128)(2,1)} %copy-done.7) | copy-start | bytes 4718596
  225.5 96.1 %collective-permute-start.1 = (f32[2,256]{1,0:T(2,128)S(1)}, f32[2,256]{1,0:T(2,128)S(1)}, u32[]{:S(2)}, u32[]{:S(2)}) collective-permute-start(f32[2,256]{1,0:T(2,128)S(1)} %pad_maximum_fusion.7), channel_id=1, source_target_pairs={{0,4},{4,0},{1,5},{5,1},{2,6},{6,2},{3,7},{7,3},{8,12},{12,8},{9,1... | collective-permute-start | bytes 6152 | tf_op jit(solution)/shard_map/ppermute | solution.py:471
  249.6 3.7 %copy-start.1 = (bf16[3072,1536]{1,0:T(8,128)(2,1)S(1)}, bf16[3072,1536]{1,0:T(8,128)(2,1)}, u32[]{:S(2)}) copy-start(bf16[3072,1536]{1,0:T(8,128)(2,1)} %copy.42) | copy-start | bytes 28311556
  253.3 68.3 %copy-start.9 = (bf16[256,3072]{1,0:T(8,128)(2,1)S(1)}, bf16[256,3072]{1,0:T(8,128)(2,1)}, u32[]{:S(2)}) copy-start(bf16[256,3072]{1,0:T(8,128)(2,1)} %copy-done.7) | copy-start | bytes 4718596
  319.8 2.3 copy-start.4
Sparse Core Ops, SparseCore 0:
  91.9 35.5 all-gather.1
  150.8 34.2 reduce-scatter.1

commit v3 on v2

--- a/solution.py
+++ b/solution.py
@@ -471,17 +471,10 @@
         return lax.ppermute(values, "tensor", pairs)
 
     inner_low = inner_grad.astype(jnp.bfloat16)
-    share = share_of(inner_low, tensor_at).astype(jnp.float32)
-    for step in range(1, tensor_count):
-        sent = share_of(inner_low, (tensor_at + step) % tensor_count)
-        share = share + shifted(sent, step).astype(jnp.float32)
-    unit_share = share_of(normed, tensor_at)
-    own_sums = jnp.stack([jnp.sum(share, axis=-1), jnp.sum(share * unit_share, axis=-1)])
-    both_sums = own_sums
-    for step in range(1, tensor_count):
-        both_sums = both_sums + shifted(own_sums, step)
-    means = both_sums[:, :, None] / feature_count
-    branch = (share - means[0] - unit_share * means[1]) * inverse
+    arrived = [
+        shifted(share_of(inner_low, (tensor_at + step) % tensor_count), step)
+        for step in range(1, tensor_count)
+    ]
     left_rows = unit_low
     right_rows = grad_rows
     qkv_term = jnp.einsum(
@@ -490,9 +483,20 @@
     out_term = jnp.einsum(
         "rd,rc->dc", right_rows, attended_flat, preferred_element_type=jnp.float32
     ).astype(jnp.bfloat16)
-    summed = scatter_rows(
-        jnp.concatenate([qkv_term, out_term], axis=1).reshape(-1, own_rows, 4 * column_count)
-    )
+    terms = jnp.concatenate([qkv_term, out_term], axis=1)
+    terms = terms.reshape(-1, own_rows, 4 * column_count)
+    arrived, terms = lax.optimization_barrier((arrived, terms))
+    share = share_of(inner_low, tensor_at).astype(jnp.float32)
+    for other in arrived:
+        share = share + other.astype(jnp.float32)
+    unit_share = share_of(normed, tensor_at)
+    own_sums = jnp.stack([jnp.sum(share, axis=-1), jnp.sum(share * unit_share, axis=-1)])
+    both_sums = own_sums
+    for step in range(1, tensor_count):
+        both_sums = both_sums + shifted(own_sums, step)
+    means = both_sums[:, :, None] / feature_count
+    branch = (share - means[0] - unit_share * means[1]) * inverse
+    summed = scatter_rows(terms)
     return (
         summed[:, : 3 * column_count].reshape(own_rows, 3, column_count),
         summed[:, 3 * column_count :],

time: 337 us -> 314 us (0.932)
  waiting for transfers between devices: 72.5 us -> 55.9 us
  local copies, waits for them, and re-layouts: 53 us -> 45.9 us
    ppermute x2, waiting for transfers between devices: 11.9 us -> 0.01 us  [shifted(): return lax.ppermute(values, 'tensor', pairs)]
    reduce_scatter x1, waiting for transfers between devices: 29.6 us -> 24.9 us  [local(): lax.psum_scatter(every_grad.astype(jnp.bfloat16), 'seq', scatter_dimensio...]
    unnamed x54 -> x60, local copies, waits for them, and re-layouts: 7.47 us -> 5.77 us
  transfers between devices with their start and end apart: 4 -> 4, of which waited for: 3 -> 2; matrix products, arithmetic and copies ran while one was open for 12% -> 12% of each run, Pallas kernels for 20% -> 22%
where the time goes in v3:
time: 314 us; the launch traced here: 309 us
  Pallas kernels  130 us (41%)
  waiting for transfers between devices  55.9 us (18%)
  local copies, waits for them, and re-layouts  45.9 us (15%)
  other arithmetic  30.6 us (10%)
  matrix products  29.9 us (10%)
  between operations  14.5 us (5%)
    pallas_call x1, Pallas kernels, scatter_rows(): pl.pallas_call(functools.partial(scatter_kernel, seq_count, dp_count), ou...  66.5 us
    pallas_call x1, Pallas kernels, gather_rows(): pl.pallas_call(functools.partial(gather_kernel, seq_count, dp_count), out...  63.3 us
    all_gather x1, waiting for transfers between devices, local(): every_pair = lax.all_gather(key_value, 'seq', axis=1, tiled=True)  31 us
    reduce_scatter x1, waiting for transfers between devices, local(): lax.psum_scatter(every_grad.astype(jnp.bfloat16), 'seq', scatter_dimensio...  24.9 us
    concatenate x1, local copies, waits for them, and re-layouts, local(): terms = jnp.concatenate([qkv_term, out_term], axis=1)  12.8 us
    concatenate x1, other arithmetic, local(): terms = jnp.concatenate([qkv_term, out_term], axis=1)  9.91 us
  transfers between devices with their start and end apart: 4, of which 2 were waited for; matrix products, arithmetic and copies ran while one was open for 12% of the time, Pallas kernels for 22%

profile of v3, /device:TPU:0, one launch (start us, length us, event | category | flops | bytes accessed | tf_op | source)
XLA Modules:
  0.0 309.0 jit_solution(13360908511394105224)
XLA Ops:
  7.2 0.0 all-gather.2.cloned.1.call-start
  7.2 1.2 copy.49
  8.4 1.8 pad_maximum_fusion.2.own_ref
  10.2 63.3 %gather_rows.1 = bf16[16,192,1536]{2,1,0:T(8,128)(2,1)} custom-call(bf16[192,1536]{1,0:T(8,128)(2,1)} %pad_maximum_fusion.2.own_ref), custom_call_target="tpu_custom_call" | custom-call | bytes 150000000 | tf_op jit(solution)/shard_map/gather_rows/pallas_call | solution.py:154
  73.5 0.3 convert_reduce_fusion
  73.8 0.6 fusion.11
  74.4 5.3 %fusion.2 = f32[256,1152]{1,0:T(8,128)S(1)} fusion(bf16[3072,1536]{1,0:T(8,128)(2,1)} %bitcast.99, bf16[1,256,3072]{2,1,0:T(8,128)(2,1)S(1)} %copy-done.3, f32[256]{0:T(256)S(1)} %add_rsqrt_fusion.2, f32[256]{0:T(256)S(1)} %broadcast_multiply_fusion.6), kind=kOutput, calls=%fused_computation.4 | convolution fusion | flops 1815085056 | bytes 9832448 | tf_op jit(solution)/shard_map/dot_general | solution.py:383
  79.7 0.8 fusion.50
  80.4 0.3 copy-done.18
  80.8 0.8 slice.64
  81.5 1.2 copy.25
  82.8 0.1 multiply_reduce_fusion.5
  82.8 0.8 mul.131
  83.6 1.9 copy.27
  85.5 0.8 sub.84
  86.3 1.9 copy.26
  88.2 2.2 fusion.62
  90.4 1.7 pad_maximum_fusion.4
  92.1 0.0 all-gather.2.cloned.1.call-update
  92.2 0.2 reduce-scatter.2.cloned.1.call-start
  92.4 1.2 copy.29
  93.6 0.1 multiply_reduce_fusion.4
  93.7 3.2 %fusion.37 = bf16[384,256]{1,0:T(8,128)(2,1)} fusion(bf16[1,256,3072]{2,1,0:T(8,128)(2,1)S(1)} %copy-done, bf16[3072,1536]{1,0:T(8,128)(2,1)} %bitcast.100), kind=kOutput, calls=%fused_computation.39 | convolution fusion | flops 604078080 | bytes 4128768 | tf_op jit(solution)/shard_map/dot_general | solution.py:384
  96.9 31.0 %all-gather.2.cloned.1.call-done = bf16[2,1024,384]{2,1,0:T(8,128)(2,1)} async-done(((bf16[2,256,384]{2,1,0:T(8,128)(2,1)}), bf16[2,1024,384]{2,1,0:T(8,128)(2,1)}) %all-gather.2.cloned.1.call-update) | async-done | bytes 1572880 | tf_op jit(solution)/shard_map/all_gather | solution.py:414
  127.8 2.7 fusion.61
  130.5 2.3 copy.28
  132.8 2.0 fusion.14
  134.8 1.9 fusion.24
  136.7 2.3 copy.36
  139.0 2.3 copy.32
  141.3 3.6 %multiply_reduce_fusion.3 = (f32[256,3]{0,1:T(4,128)S(1)}, bf16[256,3,128]{0,2,1:T(8,128)(2,1)}) fusion(bf16[256,3,128]{0,2,1:T(8,128)(2,1)} %bitcast.129, f32[256,3]{0,1:T(4,128)} %bitcast.126, bf16[1024,3,128]{0,2,1:T(8,128)(2,1)} %bitcast.116, f32[3,256,1024]{2,1,0:T(8,128)} %copy-done.16), kind=kOutput, calls=%fused_computation.55 | convolution fusion | flops 203488512 | bytes 4331520 | tf_op jit(solution)/shard_map/hqk,khd->qhd/dot_general | solution.py:418
  144.9 1.1 multiply_convert_fusion
  146.1 1.2 copy-done.10
  147.2 1.3 convolution_convert_fusion.2
  148.5 2.3 copy.35
  150.8 2.8 pad_maximum_fusion.1
  153.6 0.0 reduce-scatter.2.cloned.1.call-update
  153.7 3.1 %fusion.9 = f32[256,3072]{1,0:T(8,128)} fusion(bf16[1,256,3072]{2,1,0:T(8,128)(2,1)S(1)} %copy-done.3, f32[256]{0:T(256)} %copy-done.22, f32[256]{0:T(256)} %copy-done.24), kind=kLoop, calls=%fused_computation.12 | loop fusion | flops 2359296 | bytes 4720640 | tf_op jit(solution)/shard_map/mul | solution.py:355
  156.8 0.7 fusion.60
  157.4 0.8 multiply_convert_fusion.2
  158.2 1.8 copy.41
  160.0 3.2 %fusion.4 = bf16[3072,384]{0,1:T(8,128)(2,1)} fusion(bf16[256,384]{0,1:T(8,128)(2,1)} %bitcast.121, bf16[1,256,3072]{2,1,0:T(8,128)(2,1)S(1)} %copy-done), kind=kOutput, calls=%fused_computation.9 | convolution fusion | flops 605159424 | bytes 4128768 | tf_op jit(solution)/shard_map/rd,rc->dc/dot_general | solution.py:483
  163.2 24.9 %reduce-scatter.2.cloned.1.call-done = bf16[2,256,384]{2,1,0:T(8,128)(2,1)} async-done(((bf16[2,1024,384]{2,1,0:T(8,128)(2,1)}), bf16[2,256,384]{2,1,0:T(8,128)(2,1)}) %reduce-scatter.2.cloned.1.call-update) | async-done | bytes 393232 | tf_op jit(solution)/shard_map/reduce_scatter | solution.py:448
  188.1 1.7 slice_convert_fusion.1
  189.8 0.2 copy.37
  190.0 0.1 multiply_reduce_fusion.1
  190.1 0.2 copy.38
  190.4 0.2 copy.39
  190.6 1.2 fusion.48
  191.9 5.3 %fusion.5 = bf16[256,3072]{1,0:T(8,128)(2,1)S(1)} fusion(bf16[3072,1536]{1,0:T(8,128)(2,1)} %bitcast.101, bf16[256,384]{1,0:T(8,128)(2,1)S(1)} %copy-done.21, bf16[256,384]{1,0:T(8,128)(2,1)S(1)} %fusion.48, bf16[256,384]{1,0:T(8,128)(2,1)S(1)} %copy-done.20), kind=kOutput, calls=%fused_computation.10 | convolution fusion | flops 1814495232 | bytes 9240576 | tf_op jit(solution)/shard_map/rc,dc->rd/dot_general | solution.py:461
  197.2 2.4 convolution_convert_fusion
  199.6 0.9 constant_dynamic-slice_fusion
  200.6 1.5 collective-permute-start
  202.0 9.9 %pad_maximum_fusion = bf16[3072,1536]{0,1:T(8,128)(2,1)} fusion(bf16[3072,384]{0,1:T(8,128)(2,1)S(1)} %copy-done.4, bf16[3072,1152]{0,1:T(8,128)(2,1)S(1)} %convolution_convert_fusion), kind=kLoop, calls=%fused_computation.1 | loop fusion | flops 18874368 | bytes 18874368 | tf_op jit(solution)/shard_map/concatenate | solution.py:486
  212.0 12.8 %copy.42 = bf16[3072,1536]{1,0:T(8,128)(2,1)} copy(bf16[3072,1536]{0,1:T(8,128)(2,1)} %pad_maximum_fusion) | data formatting | bytes 18874368 | tf_op jit(solution)/shard_map/concatenate | solution.py:486
  224.8 1.8 fusion.27
  226.6 0.6 collective-permute-start.1
  227.2 3.7 %copy-done.2 = bf16[3072,1536]{1,0:T(8,128)(2,1)S(1)} copy-done((bf16[3072,1536]{1,0:T(8,128)(2,1)S(1)}, bf16[3072,1536]{1,0:T(8,128)(2,1)}, u32[]{:S(2)}) %copy-start.2) | copy-done | bytes 9437208
  230.9 66.5 %scatter_rows.1 = f32[192,1536]{1,0:T(8,128)S(1)} custom-call(bf16[16,192,1536]{2,1,0:T(8,128)(2,1)S(1)} %bitcast.92), custom_call_target="tpu_custom_call" | custom-call | bytes 180000000 | tf_op jit(solution)/shard_map/scatter_rows/pallas_call | solution.py:322
  297.4 0.1 slice.59
  297.5 0.7 slice.60
  298.2 1.0 copy.51
  299.2 0.5 copy-done.6
  299.7 2.4 fusion.43
  (73 shorter events, 0.3 us)
Async XLA Ops:
  7.2 86.5 %copy-start = (bf16[1,256,3072]{2,1,0:T(8,128)(2,1)S(1)}, bf16[1,256,3072]{2,1,0:T(8,128)(2,1)}, u32[]{:S(2)}) copy-start(bf16[1,256,3072]{2,1,0:T(8,128)(2,1)} %param.5) | copy-start | bytes 4718596
  7.2 120.7 %all-gather.2.cloned.1.call-start = ((), (), s32[]{:S(2)}) async-start(), calls=%async_computation.1 | async-start | bytes 1966080 | tf_op jit(solution)/shard_map/all_gather | solution.py:414
  10.2 63.3 %copy-start.3 = (bf16[1,256,3072]{2,1,0:T(8,128)(2,1)S(1)}, bf16[1,256,3072]{2,1,0:T(8,128)(2,1)}, u32[]{:S(2)}) copy-start(bf16[1,256,3072]{2,1,0:T(8,128)(2,1)} %param.4) | copy-start | bytes 4718596
  73.8 5.9 %copy-start.24 = (f32[256]{0:T(256)}, f32[256]{0:T(256)S(1)}, u32[]{:S(2)}) copy-start(f32[256]{0:T(256)S(1)} %broadcast_multiply_fusion.6) | copy-start | bytes 3076
  74.4 5.3 %copy-start.22 = (f32[256]{0:T(256)}, f32[256]{0:T(256)S(1)}, u32[]{:S(2)}) copy-start(f32[256]{0:T(256)S(1)} %add_rsqrt_fusion.2) | copy-start | bytes 3076
  79.7 1.1 copy-start.18
  82.7 7.7 %copy-start.8 = (f32[256,384]{0,1:T(8,128)}, f32[256,384]{0,1:T(8,128)S(1)}, u32[]{:S(2)}) copy-start(f32[256,384]{0,1:T(8,128)S(1)} %copy.25) | copy-start | bytes 1179652
  92.2 95.9 %reduce-scatter.2.cloned.1.call-start = ((), (), s32[]{:S(2)}) async-start(), calls=%async_computation.2 | async-start | bytes 1966080 | tf_op jit(solution)/shard_map/reduce_scatter | solution.py:448
  132.8 2.0 copy-start.28
  134.8 1.9 copy-start.16
  134.8 1.9 copy-start.26
  141.3 3.6 %copy-start.17 = (f32[3,256,1024]{2,1,0:T(8,128)S(1)}, f32[3,256,1024]{2,1,0:T(8,128)}, u32[]{:S(2)}) copy-start(f32[3,256,1024]{2,1,0:T(8,128)} %copy-done.16) | copy-start | bytes 9437188
  141.3 3.6 %copy-start.19 = (bf16[1,1024,384]{1,2,0:T(8,128)(2,1)S(1)}, bf16[1,1024,384]{1,2,0:T(8,128)(2,1)}, u32[]{:S(2)}) copy-start(bf16[1,1024,384]{1,2,0:T(8,128)(2,1)} %copy.32) | copy-start | bytes 2359300
  141.3 3.6 %copy-start.27 = (f32[3,256]{1,0:T(4,128)S(1)}, f32[3,256]{1,0:T(4,128)}, u32[]{:S(2)}) copy-start(f32[3,256]{1,0:T(4,128)} %copy-done.26) | copy-start | bytes 9220
  141.3 3.6 %copy-start.29 = (bf16[384,256]{1,0:T(8,128)(2,1)S(1)}, bf16[384,256]{1,0:T(8,128)(2,1)}, u32[]{:S(2)}) copy-start(bf16[384,256]{1,0:T(8,128)(2,1)} %fusion.37) | copy-start | bytes 589828
  146.1 1.2 copy-start.10
  153.6 3.1 %copy-start.7 = (bf16[1,1024,384]{1,2,0:T(8,128)(2,1)S(1)}, bf16[1,1024,384]{1,2,0:T(8,128)(2,1)}, u32[]{:S(2)}) copy-start(bf16[1,1024,384]{1,2,0:T(8,128)(2,1)} %copy.28) | copy-start | bytes 2359300
  153.6 3.1 %copy-start.11 = (bf16[3,256,1024]{2,1,0:T(8,128)(2,1)S(1)}, bf16[3,256,1024]{2,1,0:T(8,128)(2,1)}, u32[]{:S(2)}) copy-start(bf16[3,256,1024]{2,1,0:T(8,128)(2,1)} %copy-done.10) | copy-start | bytes 4718596
  160.0 30.0 %copy-start.9 = (f32[256,384]{0,1:T(8,128)S(1)}, f32[256,384]{0,1:T(8,128)}, u32[]{:S(2)}) copy-start(f32[256,384]{0,1:T(8,128)} %copy-done.8) | copy-start | bytes 1179652
  163.2 27.4 %copy-start.14 = (f32[256,384]{1,0:T(8,128)S(1)}, f32[256,384]{1,0:T(8,128)}, u32[]{:S(2)}) copy-start(f32[256,384]{1,0:T(8,128)} %copy.27) | copy-start | bytes 1179652
  163.2 27.4 %copy-start.15 = (f32[256,384]{1,0:T(8,128)S(1)}, f32[256,384]{1,0:T(8,128)}, u32[]{:S(2)}) copy-start(f32[256,384]{1,0:T(8,128)} %copy.26) | copy-start | bytes 1179652
  190.5 1.3 copy-start.20
  190.6 1.3 copy-start.21
  191.8 5.3 %copy-start.23 = (f32[256]{0:T(256)S(1)}, f32[256]{0:T(256)}, u32[]{:S(2)}) copy-start(f32[256]{0:T(256)} %copy-done.22) | copy-start | bytes 3076
  191.8 5.3 %copy-start.25 = (f32[256]{0:T(256)S(1)}, f32[256]{0:T(256)}, u32[]{:S(2)}) copy-start(f32[256]{0:T(256)} %copy-done.24) | copy-start | bytes 3076
  197.2 2.4 copy-start.12
  197.2 4.8 %copy-start.4 = (bf16[3072,384]{0,1:T(8,128)(2,1)S(1)}, bf16[3072,384]{0,1:T(8,128)(2,1)}, u32[]{:S(2)}) copy-start(bf16[3072,384]{0,1:T(8,128)(2,1)} %fusion.4) | copy-start | bytes 7077892
  200.6 24.2 %collective-permute-start = (bf16[256,1536]{1,0:T(8,128)(2,1)}, bf16[256,1536]{1,0:T(8,128)(2,1)}, u32[]{:S(2)}, u32[]{:S(2)}) collective-permute-start(bf16[256,1536]{1,0:T(8,128)(2,1)} %constant_dynamic-slice_fusion), channel_id=1, source_target_pairs={{0,4},{4,0},{1,5},{5,1},{2,6},{6,2},{3,7},{7,3},{8,12},{12,8},{9,1... | collective-permute-start | bytes 2359304 | tf_op jit(solution)/shard_map/ppermute | solution.py:471
  212.0 12.8 %copy-start.5 = (f32[256,3072]{1,0:T(8,128)S(1)}, f32[256,3072]{1,0:T(8,128)}, u32[]{:S(2)}) copy-start(f32[256,3072]{1,0:T(8,128)} %fusion.9) | copy-start | bytes 9437188
  226.6 72.6 %collective-permute-start.1 = (f32[2,256]{1,0:T(2,128)S(1)}, f32[2,256]{1,0:T(2,128)S(1)}, u32[]{:S(2)}, u32[]{:S(2)}) collective-permute-start(f32[2,256]{1,0:T(2,128)S(1)} %pad_maximum_fusion.7), channel_id=1, source_target_pairs={{0,4},{4,0},{1,5},{5,1},{2,6},{6,2},{3,7},{7,3},{8,12},{12,8},{9,1... | collective-permute-start | bytes 6152 | tf_op jit(solution)/shard_map/ppermute | solution.py:471
  227.2 3.7 %copy-start.2 = (bf16[3072,1536]{1,0:T(8,128)(2,1)S(1)}, bf16[3072,1536]{1,0:T(8,128)(2,1)}, u32[]{:S(2)}) copy-start(bf16[3072,1536]{1,0:T(8,128)(2,1)} %copy.42) | copy-start | bytes 28311556
  230.9 68.3 %copy-start.13 = (bf16[256,3072]{1,0:T(8,128)(2,1)S(1)}, bf16[256,3072]{1,0:T(8,128)(2,1)}, u32[]{:S(2)}) copy-start(bf16[256,3072]{1,0:T(8,128)(2,1)} %copy-done.12) | copy-start | bytes 4718596
  297.4 2.3 copy-start.6
  298.2 3.9 %copy-start.1 = (bf16[1,256,3072]{2,1,0:T(8,128)(2,1)S(1)}, bf16[1,256,3072]{2,1,0:T(8,128)(2,1)}, u32[]{:S(2)}) copy-start(bf16[1,256,3072]{2,1,0:T(8,128)(2,1)} %param.5) | copy-start | bytes 4718596
Sparse Core Ops, SparseCore 0:
  92.3 35.5 all-gather.1
  153.7 34.2 reduce-scatter.1
